TPU v7x, 512 devices: a whole 4x4x16 slice. The times are simulated.
512 devices in a mesh: row: 8 (over z_hi, core), col: 16 (over y, z_lo), dp: 4 (over x).
Axes of the slice: x: 4, y: 4, z: 16 (z_hi: 4, z_lo: 4; z = z_hi * 4 + z_lo), core: 2. Of those that a mesh axis runs over, the one named last changes fastest.
Arguments:
- activations: bfloat16 [4, 1024, 16384], P('dp', 'col', 'row'), may hold values from -6 to 6
- out_grads: bfloat16 [4, 1024, 4096], P('dp', 'row', 'col'), may hold values from -6 to 6
- block_mask: int32 [128, 32], P('row', 'col'), may hold values from 0 to 1, as said below
- master_weight: float32 [16384, 4096], P(('row', 'dp'), 'col'), may hold values from -0.046875 to 0.046875
- first_moment: float32 [16384, 4096], P(('row', 'dp'), 'col'), may hold values from -12 to 12
- second_moment: float32 [16384, 4096], P(('row', 'dp'), 'col'), may hold values from 0.05 to 2
Outputs:
- input_grads: bfloat16 [4, 1024, 16384], P('dp', 'col', 'row')
- new_weight: float32 [16384, 4096], P(('row', 'dp'), 'col')
- new_first: float32 [16384, 4096], P(('row', 'dp'), 'col')
- new_second: float32 [16384, 4096], P(('row', 'dp'), 'col')
Inputs may be any that keep to these rules, and one draw needn't show every extreme that they name: `block_mask`: 1 where the 128 x 128 block of the weight is kept, 0 where it is pruned.
All inputs are finite; a program needn't handle non-finite values.
Results may differ from a plain program's by a relative error of at most 0.015.
Values may be sent and summed in bfloat16 or wider, within the bound.
No kernel may reach another device: no remote copies, remote signals or barrier semaphores. Data moves between devices by JAX's collectives and lax.ppermute only.
A program may use at most 64 MiB of HBM per device.

v0:
```python
import jax
import jax.numpy as jnp
from jax import lax
from jax.sharding import Mesh
from jax.sharding import PartitionSpec as P

BLOCK = 128
ROW = ("row_0", "row_1")
ROW_DP = ("row_0", "row_1", "dp")
first_decay = 0.9
second_decay = 0.999
learn_rate = 0.001
adam_epsilon = 1e-08
first_correct = 1.0 - 0.9**10
second_correct = 1.0 - 0.999**10


def from_everyone(array, axis):
    copies = jnp.broadcast_to(array, (lax.axis_size(axis), *array.shape))
    return lax.all_to_all(copies, axis, split_axis=0, concat_axis=0, tiled=True)


def in_order(pieces, dim):
    dims = list(pieces.shape[1:])
    dims[dim] *= pieces.shape[0]
    return jnp.moveaxis(pieces, 0, dim).reshape(dims)


def gather_directly(array, axis, dim):
    pieces = from_everyone(array, axis)
    return in_order(pieces, dim)


def stacked_from(array, axes, sequence):
    pieces = array
    for k in sequence:
        pieces = lax.all_gather(pieces, axes[k])
    done = sequence[::-1]
    back = [done.index(k) for k in range(len(axes))]
    pieces = pieces.transpose(*back, *range(len(axes), pieces.ndim))
    return pieces.reshape(-1, *array.shape)


def gathered_by_axis(array, axes, sequence, dim):
    return in_order(stacked_from(array, axes, sequence), dim)


def split_up(array, dim, peers):
    before, after = (array.shape[:dim], array.shape[dim + 1 :])
    return jnp.moveaxis(array.reshape(*before, peers, -1, *after), dim, 0)


def summed_on_arrival(array, axis, dim):
    peers = lax.axis_size(axis)
    pieces = lax.all_to_all(split_up(array, dim, peers), axis, 0, 0, tiled=True)
    return jnp.sum(pieces.astype(jnp.float32), axis=0)


def expand(block_keep):
    tall, broad = block_keep.shape
    values = block_keep.astype(jnp.float32)
    grown = jnp.broadcast_to(values[:, None, :, None], (tall, BLOCK, broad, BLOCK))
    return grown.reshape(tall * BLOCK, broad * BLOCK)


def body(activations, out_grads, block_mask, master_weight, first_moment, second_moment):
    shard_rows = master_weight.shape[0]
    group_index = lax.axis_index("dp")
    keep_tile = expand(block_mask)
    keep_shard = lax.dynamic_slice_in_dim(keep_tile, group_index * shard_rows, shard_rows, 0)
    weight_tile = gather_directly(master_weight.astype(jnp.bfloat16), "dp", 0)
    weight_tile = weight_tile * keep_tile.astype(jnp.bfloat16)
    grad_group = gathered_by_axis(out_grads[0], ROW, (0, 1), 0)
    picked = grad_group
    tile_grad = (
        lax.dot_general(
            lax.all_gather(activations[0], "col", axis=0, tiled=True),
            picked,
            (((0,), (0,)), ((), ())),
            preferred_element_type=jnp.float32,
        )
        * keep_tile
    )
    grads_after, tile_grad = lax.optimization_barrier((grad_group, tile_grad))
    picked = grads_after
    summed_inputs = lax.psum_scatter(
        lax.dot_general(
            picked, weight_tile, (((1,), (1,)), ((), ())), preferred_element_type=jnp.float32
        ).astype(jnp.bfloat16),
        "col",
        scatter_dimension=0,
        tiled=True,
    )
    input_grads = summed_inputs[None]
    grad_shard = summed_on_arrival(tile_grad.astype(jnp.bfloat16), "dp", 0)
    new_first = first_decay * first_moment + (1.0 - first_decay) * grad_shard
    new_second = second_decay * second_moment + (1.0 - second_decay) * grad_shard * grad_shard
    step_size = new_first / first_correct / (jnp.sqrt(new_second / second_correct) + adam_epsilon)
    new_weight = keep_shard * (master_weight - learn_rate * step_size)
    return (input_grads, new_weight, new_first, new_second)


def solution(mesh):
    finer = Mesh(
        mesh.devices.reshape(4, 2, mesh.shape["col"], mesh.shape["dp"]),
        ("row_0", "row_1", "col", "dp"),
    )
    in_specs = (
        P("dp", "col", ROW),
        P("dp", ROW, "col"),
        P(ROW, "col"),
        P(ROW_DP, "col"),
        P(ROW_DP, "col"),
        P(ROW_DP, "col"),
    )
    out_specs = (P("dp", "col", ROW), P(ROW_DP, "col"), P(ROW_DP, "col"), P(ROW_DP, "col"))
    return jax.shard_map(body, mesh=finer, in_specs=in_specs, out_specs=out_specs, check_vma=False)
```

profile of v0, /device:TPU:2, one launch (start us, length us, event | category | flops | bytes accessed | tf_op | source)
XLA Modules:
  0.0 281.5 jit_solution(17840305256738993621)
XLA Ops:
  7.2 0.0 copy-start.2
  7.2 0.0 all-gather.4.cloned.1.call-start
  7.2 0.7 all-gather.4.cloned.1.call-update
  7.9 27.1 %all_gather.12 = bf16[4,128,256]{2,1,0:T(8,128)(2,1)S(1)} all-gather(bf16[1,128,256]{2,1,0:T(8,128)(2,1)} %param.7), channel_id=1, replica_groups=mesh['row_0'=4,'row_1'=2,'col'=16,'dp'=4] {'row_0'}, dimensions={0}, use_global_device_ids=true | all-gather | bytes 327680 | tf_op jit(solution)/shard_map/all_gather | solution.py:37
  35.0 2.2 all-gather
  37.2 0.0 copy-done.2
  37.3 0.0 copy-start
  37.3 0.1 copy.15
  37.4 85.1 %all-gather.4.cloned.1.call-done = bf16[1,1024,2048]{2,1,0:T(8,128)(2,1)} async-done(((bf16[1,64,2048]{2,1,0:T(8,128)(2,1)}), bf16[1,1024,2048]{2,1,0:T(8,128)(2,1)}) %all-gather.4.cloned.1.call-update) | async-done | bytes 4194320 | tf_op jit(solution)/shard_map/all_gather | solution.py:77
  122.4 0.6 broadcast_in_dim.12
  123.0 4.5 %fusion.2 = bf16[2048,256]{1,0:T(8,128)(2,1)} fusion(bf16[1024,256]{1,0:T(8,128)(2,1)S(1)} %bitcast.28, bf16[1,1024,2048]{2,1,0:T(8,128)(2,1)} %all-gather.4.cloned.1.call-done, f32[256,8,2,128]{3,2,1,0:T(2,128)S(1)} %bitcast.25), kind=kOutput, calls=%fused_computation.3 | convolution fusion | flops 1074790400 | bytes 7864320 | tf_op jit(solution)/shard_map/dot_general | solution.py:76
  127.6 0.0 copy-done
  127.6 4.8 %all-to-all-start.1 = ((bf16[4,512,256]{2,1,0:T(8,128)(2,1)}), bf16[4,512,256]{2,1,0:T(8,128)(2,1)S(1)}, u32[]{:S(2)}, u32[]{:S(2)}) async-start(bf16[4,512,256]{2,1,0:T(8,128)(2,1)} %bitcast.32), calls=%async_computation.2 | async-start | bytes 2097152 | tf_op jit(solution)/shard_map/all_to_all | solution.py:55
  132.4 0.0 reduce-scatter.2.cloned.1.call-start
  132.4 1.5 copy.22
  133.9 12.2 %all-to-all-done.1 = bf16[4,512,256]{2,1,0:T(8,128)(2,1)S(1)} async-done(((bf16[4,512,256]{2,1,0:T(8,128)(2,1)}), bf16[4,512,256]{2,1,0:T(8,128)(2,1)S(1)}, u32[]{:S(2)}, u32[]{:S(2)}) %all-to-all-start.1) | async-done | bytes 1048608 | tf_op jit(solution)/shard_map/all_to_all | solution.py:55
  146.0 0.1 convert_reduce_fusion
  146.2 3.1 %subtract_multiply_fusion = (f32[512,256]{1,0:T(8,128)}, f32[512,256]{1,0:T(8,128)}, f32[512,256]{1,0:T(8,128)}, bf16[512,256]{1,0:T(8,128)(2,1)S(1)}) fusion(f32[512,256]{1,0:T(8,128)} %param.9, f32[2048,256]{1,0:T(8,128)} %bitcast.30, s32[]{:T(128)S(6)} %select_n.3, f32[512,256]{1,0:T(8,128)S(1)} %convert_reduce_fusion, f32[512,256]{1,0:T(8,128)} %param.10, ...), kind=kLoop, calls=%fused_computation.9 | loop fusion | flops 1966080 | bytes 4456452 | tf_op jit(solution)/shard_map/mul | solution.py:99
  149.3 0.1 broadcast_in_dim.13
  149.3 16.7 %all_to_all.10 = bf16[4,512,256]{2,1,0:T(8,128)(2,1)S(1)} all-to-all(bf16[4,512,256]{2,1,0:T(8,128)(2,1)S(1)} %broadcast_in_dim.13), channel_id=1, replica_groups=mesh['row_0'=4,'row_1'=2,'col'=16,'dp'=4] {'dp'}, dimensions={0} | all-to-all | bytes 2097152 | tf_op jit(solution)/shard_map/all_to_all | solution.py:20
  166.0 0.0 copy-start.1
  166.0 0.2 bitcast_multiply_fusion
  166.2 0.8 copy-done.1
  167.1 3.2 %convolution_convert_fusion = bf16[1024,2048]{1,0:T(8,128)(2,1)} fusion(bf16[1024,256]{1,0:T(8,128)(2,1)S(1)} %bitcast.29, bf16[2048,256]{1,0:T(8,128)(2,1)S(1)} %bitcast_multiply_fusion), kind=kOutput, calls=%fused_computation.2 | convolution fusion | flops 1075838976 | bytes 5767168 | tf_op jit(solution)/shard_map/dot_general | solution.py:87
  170.3 0.0 reduce-scatter.2.cloned.1.call-update
  170.3 104.3 %reduce-scatter.2.cloned.1.call-done = bf16[64,2048]{1,0:T(8,128)(2,1)} async-done(((bf16[1024,2048]{1,0:T(8,128)(2,1)}), bf16[64,2048]{1,0:T(8,128)(2,1)}) %reduce-scatter.2.cloned.1.call-update) | async-done | bytes 262160 | tf_op jit(solution)/shard_map/reduce_scatter | solution.py:86
  (2 shorter events, 0.0 us)
Async XLA Ops:
  7.2 30.1 %copy-start.2 = (s32[16,2]{0,1:T(2,128)S(1)}, s32[16,2]{0,1:T(2,128)}, u32[]{:S(2)}) copy-start(s32[16,2]{0,1:T(2,128)} %param.8) | copy-start | bytes 388
  7.2 115.2 %all-gather.4.cloned.1.call-start = ((), (), s32[]{:S(2)}) async-start(), calls=%async_computation.4 | async-start | bytes 4456448 | tf_op jit(solution)/shard_map/all_gather | solution.py:77
  37.3 90.3 %copy-start = (bf16[4,2,128,256]{3,2,1,0:T(8,128)(2,1)}, bf16[4,2,128,256]{3,2,1,0:T(8,128)(2,1)S(1)}, u32[]{:S(2)}) copy-start(bf16[4,2,128,256]{3,2,1,0:T(8,128)(2,1)S(1)} %copy.14) | copy-start | bytes 1572868
  127.6 18.5 %all-to-all-start.1 = ((bf16[4,512,256]{2,1,0:T(8,128)(2,1)}), bf16[4,512,256]{2,1,0:T(8,128)(2,1)S(1)}, u32[]{:S(2)}, u32[]{:S(2)}) async-start(bf16[4,512,256]{2,1,0:T(8,128)(2,1)} %bitcast.32), calls=%async_computation.2 | async-start | bytes 2097152 | tf_op jit(solution)/shard_map/all_to_all | solution.py:55
  132.4 142.2 %reduce-scatter.2.cloned.1.call-start = ((), (), s32[]{:S(2)}) async-start(), calls=%async_computation.3 | async-start | bytes 4456448 | tf_op jit(solution)/shard_map/reduce_scatter | solution.py:86
  166.0 1.0 copy-start.1
Sparse Core Ops, SparseCore 0:
  10.1 112.3 all-gather.3
  170.4 104.1 reduce-scatter.1
where the time goes:
time: 282 us; the launch traced here: 281 us
  waiting for transfers between devices  202 us (72%)
  blocking collectives  46 us (16%)
  between operations  14.1 us (5%)
  matrix products  7.77 us (3%)
  starting transfers between devices  4.84 us (2%)
  other arithmetic  3.41 us (1%)
  local copies, waits for them, and re-layouts  3.12 us (1%)
    reduce_scatter x1, waiting for transfers between devices, body(): lax.psum_scatter(lax.dot_general(picked, weight_tile, (((1,), (1,)), ((),...  104 us
    all_gather x1, waiting for transfers between devices, body(): lax.all_gather(activations[0], 'col', axis=0, tiled=True)  85.1 us
    all_gather x2, blocking collectives, stacked_from(): pieces = lax.all_gather(pieces, axes[k])  29.3 us
    all_to_all x1, blocking collectives, from_everyone(): return lax.all_to_all(copies, axis, split_axis=0, concat_axis=0, tiled=True)  16.7 us
    all_to_all x1, waiting for transfers between devices, summed_on_arrival(): pieces = lax.all_to_all(split_up(array, dim, peers), axis, 0, 0, tiled=True)  12.2 us
  transfers between devices with their start and end apart: 3, of which 3 were waited for; matrix products, arithmetic and copies ran while one was open for 1% of the time, Pallas kernels for 0%

commit v1 on v0

--- a/solution.py
+++ b/solution.py
@@ -74,7 +74,10 @@
     picked = grad_group
     tile_grad = (
         lax.dot_general(
-            lax.all_gather(activations[0], "col", axis=0, tiled=True),
+            jnp.concatenate(
+                lax.all_to_all(jnp.stack([activations[0]] * lax.axis_size("col")), "col", 0, 0),
+                axis=0,
+            ),
             picked,
             (((0,), (0,)), ((), ())),
             preferred_element_type=jnp.float32,

time: 282 us -> 299 us (1.060)
  the two profiles are of different devices: /device:TPU:2 before, /device:TPU:6 now
where the time goes in v1:
time: 299 us; the launch traced here: 298 us
  waiting for transfers between devices  146 us (49%)
  blocking collectives  107 us (36%)
  between operations  14.1 us (5%)
  starting transfers between devices  13.6 us (5%)
  matrix products  7.78 us (3%)
  local copies, waits for them, and re-layouts  6.57 us (2%)
  other arithmetic  3.42 us (1%)
    reduce_scatter x1, waiting for transfers between devices, body(): lax.psum_scatter(lax.dot_general(picked, weight_tile, (((1,), (1,)), ((),...  124 us
    all_gather x2, blocking collectives, stacked_from(): pieces = lax.all_gather(pieces, axes[k])  91.1 us
    all_to_all x1, blocking collectives, from_everyone(): return lax.all_to_all(copies, axis, split_axis=0, concat_axis=0, tiled=True)  15.6 us
    all_to_all x1, waiting for transfers between devices, body(): lax.all_to_all(jnp.stack([activations[0]] * lax.axis_size('col')), 'col',...  12 us
    all_to_all x1, waiting for transfers between devices, summed_on_arrival(): pieces = lax.all_to_all(split_up(array, dim, peers), axis, 0, 0, tiled=True)  10.5 us
    all_to_all x1, starting transfers between devices, body(): lax.all_to_all(jnp.stack([activations[0]] * lax.axis_size('col')), 'col',...  8.82 us
  transfers between devices with their start and end apart: 3, of which 3 were waited for; matrix products, arithmetic and copies ran while one was open for 1% of the time, Pallas kernels for 0%

profile of v1, /device:TPU:6, one launch (start us, length us, event | category | flops | bytes accessed | tf_op | source)
XLA Modules:
  0.0 298.3 jit_solution(3683302855720982733)
XLA Ops:
  7.2 3.4 %stack.3 = bf16[16,64,2048]{2,1,0:T(8,128)(2,1)} broadcast(bf16[64,2048]{1,0:T(8,128)(2,1)} %bitcast.31), dimensions={1,2} | broadcast | bytes 4456448 | tf_op jit(solution)/shard_map/stack | solution.py:78
  10.6 0.0 copy-start.2
  10.6 8.8 %all-to-all-start = ((bf16[16,64,2048]{2,1,0:T(8,128)(2,1)}), bf16[16,64,2048]{2,1,0:T(8,128)(2,1)}, u32[]{:S(2)}, u32[]{:S(2)}) async-start(bf16[16,64,2048]{2,1,0:T(8,128)(2,1)} %stack.3), calls=%async_computation | async-start | bytes 8388608 | tf_op jit(solution)/shard_map/all_to_all | solution.py:78
  19.4 0.0 copy-done.2
  19.4 0.0 copy-start.3
  19.5 88.9 %all_gather.9 = bf16[4,128,256]{2,1,0:T(8,128)(2,1)S(1)} all-gather(bf16[1,128,256]{2,1,0:T(8,128)(2,1)S(1)} %copy-done.2), channel_id=1, replica_groups=mesh['row_0'=4,'row_1'=2,'col'=16,'dp'=4] {'row_0'}, dimensions={0}, use_global_device_ids=true | all-gather | bytes 327680 | tf_op jit(solution)/shard_map/all_gather | solution.py:37
  108.4 2.2 all-gather
  110.6 0.0 copy-done.3
  110.6 0.0 copy-start
  110.6 0.1 copy.15
  110.7 12.0 %all-to-all-done = bf16[16,64,2048]{2,1,0:T(8,128)(2,1)} async-done(((bf16[16,64,2048]{2,1,0:T(8,128)(2,1)}), bf16[16,64,2048]{2,1,0:T(8,128)(2,1)}, u32[]{:S(2)}, u32[]{:S(2)}) %all-to-all-start) | async-done | bytes 4194336 | tf_op jit(solution)/shard_map/all_to_all | solution.py:78
  122.6 0.6 broadcast_in_dim.12
  123.3 4.5 %convolution_multiply_fusion = bf16[2048,256]{1,0:T(8,128)(2,1)} fusion(bf16[1024,2048]{1,0:T(8,128)(2,1)} %bitcast.4, bf16[1024,256]{1,0:T(8,128)(2,1)S(1)} %bitcast.26, f32[256,8,2,128]{3,2,1,0:T(2,128)S(1)} %bitcast.23), kind=kOutput, calls=%fused_computation.1 | convolution fusion | flops 1074790400 | bytes 7864320 | tf_op jit(solution)/shard_map/dot_general | solution.py:76
  127.8 0.0 copy-done
  127.8 4.8 %all-to-all-start.2 = ((bf16[4,512,256]{2,1,0:T(8,128)(2,1)}), bf16[4,512,256]{2,1,0:T(8,128)(2,1)S(1)}, u32[]{:S(2)}, u32[]{:S(2)}) async-start(bf16[4,512,256]{2,1,0:T(8,128)(2,1)} %bitcast.30), calls=%async_computation.3 | async-start | bytes 2097152 | tf_op jit(solution)/shard_map/all_to_all | solution.py:55
  132.6 0.0 reduce-scatter.2.cloned.1.call-start
  132.6 1.5 copy.22
  134.1 10.5 %all-to-all-done.2 = bf16[4,512,256]{2,1,0:T(8,128)(2,1)S(1)} async-done(((bf16[4,512,256]{2,1,0:T(8,128)(2,1)}), bf16[4,512,256]{2,1,0:T(8,128)(2,1)S(1)}, u32[]{:S(2)}, u32[]{:S(2)}) %all-to-all-start.2) | async-done | bytes 1048608 | tf_op jit(solution)/shard_map/all_to_all | solution.py:55
  144.5 0.1 convert_reduce_fusion
  144.7 3.1 %subtract_multiply_fusion = (f32[512,256]{1,0:T(8,128)}, f32[512,256]{1,0:T(8,128)}, f32[512,256]{1,0:T(8,128)}, bf16[512,256]{1,0:T(8,128)(2,1)S(1)}) fusion(f32[512,256]{1,0:T(8,128)} %param.9, f32[2048,256]{1,0:T(8,128)} %bitcast.28, s32[]{:T(128)S(6)} %select_n.3, f32[512,256]{1,0:T(8,128)S(1)} %convert_reduce_fusion, f32[512,256]{1,0:T(8,128)} %param.10, ...), kind=kLoop, calls=%fused_computation.7 | loop fusion | flops 1966080 | bytes 4456452 | tf_op jit(solution)/shard_map/mul | solution.py:102
  147.7 0.1 broadcast_in_dim.13
  147.8 15.6 %all_to_all.15 = bf16[4,512,256]{2,1,0:T(8,128)(2,1)S(1)} all-to-all(bf16[4,512,256]{2,1,0:T(8,128)(2,1)S(1)} %broadcast_in_dim.13), channel_id=1, replica_groups=mesh['row_0'=4,'row_1'=2,'col'=16,'dp'=4] {'dp'}, dimensions={0} | all-to-all | bytes 2097152 | tf_op jit(solution)/shard_map/all_to_all | solution.py:20
  163.4 0.0 copy-start.1
  163.4 0.2 bitcast_multiply_fusion
  163.6 0.8 copy-done.1
  164.4 3.2 %convolution_convert_fusion = bf16[1024,2048]{1,0:T(8,128)(2,1)} fusion(bf16[1024,256]{1,0:T(8,128)(2,1)S(1)} %bitcast.27, bf16[2048,256]{1,0:T(8,128)(2,1)S(1)} %bitcast_multiply_fusion), kind=kOutput, calls=%fused_computation | convolution fusion | flops 1075838976 | bytes 5767168 | tf_op jit(solution)/shard_map/dot_general | solution.py:90
  167.7 0.0 reduce-scatter.2.cloned.1.call-update
  167.7 123.8 %reduce-scatter.2.cloned.1.call-done = bf16[64,2048]{1,0:T(8,128)(2,1)} async-done(((bf16[1024,2048]{1,0:T(8,128)(2,1)}), bf16[64,2048]{1,0:T(8,128)(2,1)}) %reduce-scatter.2.cloned.1.call-update) | async-done | bytes 262160 | tf_op jit(solution)/shard_map/reduce_scatter | solution.py:89
  (2 shorter events, 0.0 us)
Async XLA Ops:
  10.6 8.8 %copy-start.2 = (bf16[1,128,256]{2,1,0:T(8,128)(2,1)S(1)}, bf16[1,128,256]{2,1,0:T(8,128)(2,1)}, u32[]{:S(2)}) copy-start(bf16[1,128,256]{2,1,0:T(8,128)(2,1)} %param.7) | copy-start | bytes 196612
  10.6 112.0 %all-to-all-start = ((bf16[16,64,2048]{2,1,0:T(8,128)(2,1)}), bf16[16,64,2048]{2,1,0:T(8,128)(2,1)}, u32[]{:S(2)}, u32[]{:S(2)}) async-start(bf16[16,64,2048]{2,1,0:T(8,128)(2,1)} %stack.3), calls=%async_computation | async-start | bytes 8388608 | tf_op jit(solution)/shard_map/all_to_all | solution.py:78
  19.4 91.1 %copy-start.3 = (s32[16,2]{0,1:T(2,128)S(1)}, s32[16,2]{0,1:T(2,128)}, u32[]{:S(2)}) copy-start(s32[16,2]{0,1:T(2,128)} %param.8) | copy-start | bytes 388
  110.6 17.2 %copy-start = (bf16[4,2,128,256]{3,2,1,0:T(8,128)(2,1)}, bf16[4,2,128,256]{3,2,1,0:T(8,128)(2,1)S(1)}, u32[]{:S(2)}) copy-start(bf16[4,2,128,256]{3,2,1,0:T(8,128)(2,1)S(1)} %copy.14) | copy-start | bytes 1572868
  127.8 16.7 %all-to-all-start.2 = ((bf16[4,512,256]{2,1,0:T(8,128)(2,1)}), bf16[4,512,256]{2,1,0:T(8,128)(2,1)S(1)}, u32[]{:S(2)}, u32[]{:S(2)}) async-start(bf16[4,512,256]{2,1,0:T(8,128)(2,1)} %bitcast.30), calls=%async_computation.3 | async-start | bytes 2097152 | tf_op jit(solution)/shard_map/all_to_all | solution.py:55
  132.6 158.9 %reduce-scatter.2.cloned.1.call-start = ((), (), s32[]{:S(2)}) async-start(), calls=%async_computation.4 | async-start | bytes 4456448 | tf_op jit(solution)/shard_map/reduce_scatter | solution.py:89
  163.4 1.0 copy-start.1
Sparse Core Ops, SparseCore 0:
  167.8 123.6 reduce-scatter.1
